TPU v7x, 128 devices: a whole 4x4x4 slice. The times are simulated.
128 devices in a mesh: py: 16 (over x, y_hi, core), pz: 8 (over z, y_lo).
Axes of the slice: x: 4, y: 4 (y_hi: 2, y_lo: 2; y = y_hi * 2 + y_lo), z: 4, core: 2. Of those that a mesh axis runs over, the one named last changes fastest.
Arguments:
- velocity: float32 [3, 128, 128, 2048], P(None, ('py', 'pz')), may hold values from -6 to 6
- fluid: float32 [128, 128, 2048], P(('py', 'pz')), may hold values from 0.1 to 1
- pressure: float32 [128, 128, 2048], P(None, 'pz', 'py'), may hold values from -4 to 4
Outputs:
- projected: float32 [3, 128, 128, 2048], P(None, ('py', 'pz'))
- divergence: float32 [128, 128, 2048], P(None, 'pz', 'py')
All inputs are finite; a program needn't handle non-finite values.
Results may differ from a plain program's by a relative error of at most 0.00002.
Values sent between devices are 32-bit elements; how exact they have to be, the bound alone decides.
No kernel may reach another device: no remote copies, remote signals or barrier semaphores. Data moves between devices by JAX's collectives and lax.ppermute only.
A program may use at most 64 MiB of HBM per device.

v0:
```python
import jax
import jax.numpy as jnp
from jax import lax
from jax.sharding import PartitionSpec as P


def from_behind(shard, axis, by):
    size = lax.axis_size(axis)
    pairs = [(i, i + by) for i in range(size) if 0 <= i + by < size]
    return lax.ppermute(shard, axis, pairs)


def before_along(values, lower, axis):
    inner = lax.slice_in_dim(values, 0, values.shape[axis] - 1, axis=axis)
    return jnp.concatenate([lower, inner], axis)


def after_along(values, upper, axis):
    inner = lax.slice_in_dim(values, 1, values.shape[axis], axis=axis)
    return jnp.concatenate([inner, upper], axis)


def face_update(component, fluid, pressure, fluid_low, pressure_low, axis, first):
    index = lax.broadcasted_iota(jnp.int32, fluid.shape, axis) + first
    weight = jnp.where(
        index == 0, jnp.float32(0.0), 0.5 * (fluid + before_along(fluid, fluid_low, axis))
    )
    return weight * (component - (pressure - before_along(pressure, pressure_low, axis)))


def plane_zeros(values, axis):
    shape = list(values.shape)
    shape[axis] = 1
    return jnp.zeros(tuple(shape), jnp.float32)


def on_device(velocity, fluid, pressure):
    count_y = lax.axis_size("py")
    count_z = lax.axis_size("pz")
    x_dev = fluid.shape[0]
    depth = fluid.shape[1]
    across = fluid.shape[2]
    z_part = depth // count_z
    y_part = across // count_y
    pencil_x = pressure.shape[0]
    outgoing = pressure.reshape(count_y * count_z, pencil_x // (count_y * count_z), z_part, y_part)
    received = lax.all_to_all(outgoing, ("py", "pz"), split_axis=0, concat_axis=0, tiled=True)
    received = received.reshape(count_y, count_z, x_dev, z_part, y_part)
    slab_pressure = received.transpose(2, 1, 3, 0, 4).reshape(x_dev, depth, across)
    low_x = from_behind((fluid, slab_pressure), ("py", "pz"), 1)
    x_first = lax.axis_index(("py", "pz")) * x_dev
    z_zero = plane_zeros(fluid, 1)
    y_zero = plane_zeros(fluid, 2)
    along_x = face_update(velocity[0], fluid, slab_pressure, low_x[0], low_x[1], 0, x_first)
    along_z = face_update(velocity[1], fluid, slab_pressure, z_zero, z_zero, 1, 0)
    along_y = face_update(velocity[2], fluid, slab_pressure, y_zero, y_zero, 2, 0)
    high_x = from_behind(along_x, ("py", "pz"), -1)
    slab_div = after_along(along_x, high_x, 0) - along_x
    slab_div = slab_div + after_along(along_z, z_zero, 1) - along_z
    slab_div = slab_div + after_along(along_y, y_zero, 2) - along_y
    blocks = slab_div.reshape(x_dev, count_z, z_part, count_y, y_part)
    blocks = blocks.transpose(3, 1, 0, 2, 4).reshape(count_y * count_z, x_dev, z_part, y_part)
    arrived = lax.all_to_all(blocks, ("py", "pz"), split_axis=0, concat_axis=0, tiled=True)
    divergence = arrived.reshape(count_y * count_z * x_dev, z_part, y_part)
    projected = jnp.stack([along_x, along_z, along_y], 0)
    return (projected, divergence)


def solution(mesh):
    placed = (P(None, ("py", "pz"), None, None), P(("py", "pz"), None, None), P(None, "pz", "py"))
    return jax.shard_map(
        on_device,
        mesh=mesh,
        in_specs=placed,
        out_specs=(P(None, ("py", "pz"), None, None), P(None, "pz", "py")),
        check_vma=False,
    )
```

profile of v0, /device:TPU:1, one launch (start us, length us, event | category | flops | bytes accessed | tf_op | source)
XLA Modules:
  0.0 137.7 jit_solution(550781136157181962)
XLA Ops:
  0.6 11.5 %all-to-all-start = ((f32[128,1,16,128]{3,2,1,0:T(8,128)}), f32[128,1,16,128]{3,2,1,0:T(8,128)S(1)}, u32[]{:S(2)}, u32[]{:S(2)}) async-start(f32[128,1,16,128]{3,2,1,0:T(8,128)} %bitcast.44), calls=%async_computation | async-start | bytes 2097152 | tf_op jit(solution)/shard_map/all_to_all | solution.py:47
  12.1 3.3 %collective-permute-start = (f32[1,128,2048]{2,1,0:T(8,128)}, f32[1,128,2048]{2,1,0:T(8,128)}, u32[]{:S(2)}, u32[]{:S(2)}) collective-permute-start(f32[1,128,2048]{2,1,0:T(8,128)} %param.4), channel_id=1, source_target_pairs={{0,1},{1,2},{2,3},{3,4},{4,5},{5,6},{6,7},{7,8},{8,9},{9,10},{10,1... | collective-permute-start | bytes 3145736 | tf_op jit(solution)/shard_map/ppermute | solution.py:10
  15.4 16.4 %all-to-all-done = f32[128,1,16,128]{3,2,1,0:T(8,128)S(1)} async-done(((f32[128,1,16,128]{3,2,1,0:T(8,128)}), f32[128,1,16,128]{3,2,1,0:T(8,128)S(1)}, u32[]{:S(2)}, u32[]{:S(2)}) %all-to-all-start) | async-done | bytes 1048608 | tf_op jit(solution)/shard_map/all_to_all | solution.py:47
  31.8 0.6 copy.7
  32.4 0.2 reshape.24
  32.5 1.9 %collective-permute-start.1 = (f32[1,128,2048]{2,1,0:T(8,128)S(1)}, f32[1,128,2048]{2,1,0:T(8,128)S(1)}, u32[]{:S(2)}, u32[]{:S(2)}) collective-permute-start(f32[1,128,2048]{2,1,0:T(8,128)S(1)} %reshape.24), channel_id=1, source_target_pairs={{0,1},{1,2},{2,3},{3,4},{4,5},{5,6},{6,7},{7,8},{8,9},{9,10},{10,1... | collective-permute-start | bytes 3145736 | tf_op jit(solution)/shard_map/ppermute | solution.py:10
  34.5 11.2 %collective-permute-done = f32[1,128,2048]{2,1,0:T(8,128)} collective-permute-done((f32[1,128,2048]{2,1,0:T(8,128)}, f32[1,128,2048]{2,1,0:T(8,128)}, u32[]{:S(2)}, u32[]{:S(2)}) %collective-permute-start) | collective-permute-done | bytes 1048608 | tf_op jit(solution)/shard_map/ppermute | solution.py:10
  45.7 22.4 %collective-permute-done.1 = f32[1,128,2048]{2,1,0:T(8,128)S(1)} collective-permute-done((f32[1,128,2048]{2,1,0:T(8,128)S(1)}, f32[1,128,2048]{2,1,0:T(8,128)S(1)}, u32[]{:S(2)}, u32[]{:S(2)}) %collective-permute-start.1) | collective-permute-done | bytes 1048608 | tf_op jit(solution)/shard_map/ppermute | solution.py:10
  68.1 0.0 copy-start.2
  68.1 1.0 copy-done.2
  69.0 4.8 %fusion.2 = (f32[1,128,2048]{2,1,0:T(8,128)S(1)}, f32[1,128,2048]{2,1,0:T(8,128)S(1)}, f32[1,128,2048]{2,1,0:T(8,128)S(1)}) fusion(f32[1,128,2048]{2,1,0:T(8,128)S(1)} %reshape.24, f32[1,128,2048]{2,1,0:T(8,128)} %copy-done.2, f32[3,1,128,2048]{3,2,1,0:T(8,128)} %param.3, f32[1,128,2048]{2,1,0:T(8,128)} %param.4, f32[1,128,2048]{2,1,0:T(8,128)} %collective-permute-done, ...), kind=kLoop, calls=%fused_computation.6 | loop fusion | flops 4718592 | bytes 14664833 | tf_op jit(solution)/shard_map/mul | solution.py:28
  73.8 0.0 copy-start
  73.8 7.4 %collective-permute-start.2 = (f32[1,128,2048]{2,1,0:T(8,128)S(1)}, f32[1,128,2048]{2,1,0:T(8,128)S(1)}, u32[]{:S(2)}, u32[]{:S(2)}) collective-permute-start(f32[1,128,2048]{2,1,0:T(8,128)S(1)} %get-tuple-element.2), channel_id=1, source_target_pairs={{1,0},{2,1},{3,2},{4,3},{5,4},{6,5},{7,6},{8,7},{9,8},{10,9},{11,1... | collective-permute-start | bytes 3145736 | tf_op jit(solution)/shard_map/ppermute | solution.py:10
  81.3 0.3 slice.39
  81.6 0.1 slice.38
  81.7 21.5 %collective-permute-done.2 = f32[1,128,2048]{2,1,0:T(8,128)S(1)} collective-permute-done((f32[1,128,2048]{2,1,0:T(8,128)S(1)}, f32[1,128,2048]{2,1,0:T(8,128)S(1)}, u32[]{:S(2)}, u32[]{:S(2)}) %collective-permute-start.2) | collective-permute-done | bytes 1048608 | tf_op jit(solution)/shard_map/ppermute | solution.py:10
  103.2 0.6 subtract_bitcast_fusion
  103.8 0.0 copy-done
  103.9 0.2 copy.9
  104.0 0.0 copy-start.1
  104.1 1.3 copy.8
  105.4 11.4 %all-to-all-start.1 = ((f32[128,1,16,128]{3,2,1,0:T(8,128)}), f32[128,1,16,128]{3,2,1,0:T(8,128)}, u32[]{:S(2)}, u32[]{:S(2)}) async-start(f32[128,1,16,128]{3,2,1,0:T(8,128)} %bitcast.42), calls=%async_computation.1 | async-start | bytes 2097152 | tf_op jit(solution)/shard_map/all_to_all | solution.py:63
  116.8 0.0 copy-done.1
  116.8 1.9 %pad_maximum_fusion = f32[3,1,128,2048]{3,2,1,0:T(8,128)} fusion(f32[1,1,128,2048]{3,2,1,0:T(8,128)S(1)} %bitcast.34, f32[1,1,128,2048]{3,2,1,0:T(8,128)S(1)} %bitcast.35, f32[1,1,128,2048]{3,2,1,0:T(8,128)S(1)} %bitcast.38), kind=kLoop, calls=%fused_computation | loop fusion | flops 1572864 | bytes 6291456 | tf_op jit(solution)/shard_map/stack | solution.py:65
  118.6 16.8 %all-to-all-done.1 = f32[128,1,16,128]{3,2,1,0:T(8,128)} async-done(((f32[128,1,16,128]{3,2,1,0:T(8,128)}), f32[128,1,16,128]{3,2,1,0:T(8,128)}, u32[]{:S(2)}, u32[]{:S(2)}) %all-to-all-start.1) | async-done | bytes 1048608 | tf_op jit(solution)/shard_map/all_to_all | solution.py:63
  135.4 2.3 %copy.11 = f32[128,16,128]{2,1,0:T(8,128)} copy(f32[128,16,128]{2,1,0:T(8,128)} %bitcast.11) | data formatting | bytes 2097152
  (2 shorter events, 0.0 us)
Async XLA Ops:
  0.6 31.1 %all-to-all-start = ((f32[128,1,16,128]{3,2,1,0:T(8,128)}), f32[128,1,16,128]{3,2,1,0:T(8,128)S(1)}, u32[]{:S(2)}, u32[]{:S(2)}) async-start(f32[128,1,16,128]{3,2,1,0:T(8,128)} %bitcast.44), calls=%async_computation | async-start | bytes 2097152 | tf_op jit(solution)/shard_map/all_to_all | solution.py:47
  12.1 33.6 %collective-permute-start = (f32[1,128,2048]{2,1,0:T(8,128)}, f32[1,128,2048]{2,1,0:T(8,128)}, u32[]{:S(2)}, u32[]{:S(2)}) collective-permute-start(f32[1,128,2048]{2,1,0:T(8,128)} %param.4), channel_id=1, source_target_pairs={{0,1},{1,2},{2,3},{3,4},{4,5},{5,6},{6,7},{7,8},{8,9},{9,10},{10,1... | collective-permute-start | bytes 3145736 | tf_op jit(solution)/shard_map/ppermute | solution.py:10
  32.5 35.5 %collective-permute-start.1 = (f32[1,128,2048]{2,1,0:T(8,128)S(1)}, f32[1,128,2048]{2,1,0:T(8,128)S(1)}, u32[]{:S(2)}, u32[]{:S(2)}) collective-permute-start(f32[1,128,2048]{2,1,0:T(8,128)S(1)} %reshape.24), channel_id=1, source_target_pairs={{0,1},{1,2},{2,3},{3,4},{4,5},{5,6},{6,7},{7,8},{8,9},{9,10},{10,1... | collective-permute-start | bytes 3145736 | tf_op jit(solution)/shard_map/ppermute | solution.py:10
  68.1 1.0 copy-start.2
  73.8 30.0 %copy-start = (f32[1,128,2048]{2,1,0:T(8,128)}, f32[1,128,2048]{2,1,0:T(8,128)S(1)}, u32[]{:S(2)}) copy-start(f32[1,128,2048]{2,1,0:T(8,128)S(1)} %get-tuple-element.2) | copy-start | bytes 3145732
  73.8 29.4 %collective-permute-start.2 = (f32[1,128,2048]{2,1,0:T(8,128)S(1)}, f32[1,128,2048]{2,1,0:T(8,128)S(1)}, u32[]{:S(2)}, u32[]{:S(2)}) collective-permute-start(f32[1,128,2048]{2,1,0:T(8,128)S(1)} %get-tuple-element.2), channel_id=1, source_target_pairs={{1,0},{2,1},{3,2},{4,3},{5,4},{6,5},{7,6},{8,7},{9,8},{10,9},{11,1... | collective-permute-start | bytes 3145736 | tf_op jit(solution)/shard_map/ppermute | solution.py:10
  104.0 12.7 %copy-start.1 = (f32[1,128,2048]{2,1,0:T(8,128)S(1)}, f32[1,128,2048]{2,1,0:T(8,128)}, u32[]{:S(2)}) copy-start(f32[1,128,2048]{2,1,0:T(8,128)} %copy-done) | copy-start | bytes 3145732
  105.4 30.0 %all-to-all-start.1 = ((f32[128,1,16,128]{3,2,1,0:T(8,128)}), f32[128,1,16,128]{3,2,1,0:T(8,128)}, u32[]{:S(2)}, u32[]{:S(2)}) async-start(f32[128,1,16,128]{3,2,1,0:T(8,128)} %bitcast.42), calls=%async_computation.1 | async-start | bytes 2097152 | tf_op jit(solution)/shard_map/all_to_all | solution.py:63
where the time goes:
time: 138 us
  waiting for transfers between devices  88.2 us (64%)
  starting transfers between devices  35.5 us (26%)
  other arithmetic  7.29 us (5%)
  local copies, waits for them, and re-layouts  5.97 us (4%)
    ppermute x3, waiting for transfers between devices, from_behind(): return lax.ppermute(shard, axis, pairs)  55.1 us
    all_to_all x1, waiting for transfers between devices, on_device(): lax.all_to_all(blocks, ('py', 'pz'), split_axis=0, concat_axis=0, tiled=T...  16.8 us
    all_to_all x1, waiting for transfers between devices, on_device(): lax.all_to_all(outgoing, ('py', 'pz'), split_axis=0, concat_axis=0, tiled...  16.4 us
    ppermute x3, starting transfers between devices, from_behind(): return lax.ppermute(shard, axis, pairs)  12.6 us
    all_to_all x1, starting transfers between devices, on_device(): lax.all_to_all(outgoing, ('py', 'pz'), split_axis=0, concat_axis=0, tiled...  11.5 us
    all_to_all x1, starting transfers between devices, on_device(): lax.all_to_all(blocks, ('py', 'pz'), split_axis=0, concat_axis=0, tiled=T...  11.4 us
    mul x1, other arithmetic, face_update(): weight * (component - (pressure - before_along(pressure, pressure_low, ax...  4.78 us
    unnamed x8, local copies, waits for them, and re-layouts  3.43 us
  transfers between devices with their start and end apart: 5, of which 5 were waited for; matrix products, arithmetic and copies ran while one was open for 2% of the time, Pallas kernels for 0%

commit v1 on v0

v1 whole, which is shorter than its diff:
```python
import jax
import jax.numpy as jnp
from jax import lax
from jax.experimental import pallas as pl
from jax.experimental.pallas import tpu as pltpu
from jax.sharding import PartitionSpec as P

BOTH = ("py", "pz")
F32 = jnp.float32
HBM = pl.BlockSpec(memory_space=pltpu.HBM)
VMEM = pltpu.VMEM
DMA = pltpu.SemaphoreType.DMA


def call(kernel, outs, ins, scratch, mib, moved, **more):
    spec = {pltpu.HBM: HBM, VMEM: pl.BlockSpec(memory_space=VMEM)}
    return pl.pallas_call(
        kernel,
        out_shape=tuple(space(shape, F32) for shape, space in outs),
        in_specs=[spec[space] for _, space in ins],
        out_specs=tuple(spec[space] for _, space in outs),
        scratch_shapes=scratch,
        compiler_params=pltpu.CompilerParams(vmem_limit_bytes=mib * 1024 * 1024),
        cost_estimate=pl.CostEstimate(flops=moved, bytes_accessed=moved, transcendentals=0),
        **more,
    )(*(pltpu.with_memory_space_constraint(x, space) for x, space in ins))


def start(copies):
    for c in copies:
        c.start()


def wait(copies):
    for c in copies:
        c.wait()


def pack_kernel(f, v, p, out, sem_f, sem_v, sem_p):
    ny, ty = out.shape[0], out.shape[-1]
    copy = pltpu.make_async_copy
    loads = [copy(p, out.at[:, :, 2], sem_p)]
    for i in range(ny):
        cols = pl.ds(i * ty, ty)
        loads.append(copy(f.at[:, :, cols], out.at[i, :, 0], sem_f.at[i]))
        loads.append(copy(v.at[0, :, :, cols], out.at[i, :, 1], sem_v.at[i]))
    start(loads)
    wait(loads)


def middle_kernel(r, p_h, f_h, v_h, op, proj_h, px_h, p, f, v, zy, px, sem_p, sem_f, sem_v, sem_x, sem_zy):
    ny, nz, _, tz, ty = r.shape
    depth = nz * tz
    copy = pltpu.make_async_copy
    loads = []
    for i in range(ny):
        cols = pl.ds(i * ty, ty)
        loads.append((
            copy(p_h.at[i], p.at[i], sem_p.at[i]),
            copy(f_h.at[:, cols], f.at[i], sem_f.at[i]),
            copy(v_h.at[pl.ds(1, 2), :, cols], v.at[i], sem_v.at[i]),
        ))
        start(loads[-1])
    row = lax.broadcasted_iota(jnp.int32, (depth, ty), 0)
    lane = lax.broadcasted_iota(jnp.int32, (depth, ty), 1)
    stores = []
    before = None
    for i in range(ny):
        wait(loads[i])
        for j in range(nz):
            if i == 0 and j == 0:
                op[0, 0, 0] = px[0, 0] = jnp.zeros((tz, ty), F32)
                continue
            a, b = (i, j - 1) if j else (i - 1, nz - 1)
            weight = 0.5 * (r[i, j, 0] + r[a, b, 0])
            op[i, j, 0] = px[i, j] = weight * (r[i, j, 1] - (p[i, j] - p[a, b]))
        stores.append(copy(px.at[i], px_h.at[i], sem_x.at[i]))
        stores[-1].start()
        pres = r[i, :, 2].reshape(depth, ty)
        fluid = f[i]
        weight = jnp.where(row == 0, 0.0, 0.5 * (fluid + pltpu.roll(fluid, 1, 0)))
        pz = weight * (v[i, 0] - (pres - pltpu.roll(pres, 1, 0)))
        zy[i, 0] = pz
        dz = jnp.where(row == depth - 1, 0.0, pltpu.roll(pz, depth - 1, 0)) - pz
        rp, rf = pltpu.roll(pres, 1, 1), pltpu.roll(fluid, 1, 1)
        if i == 0:
            weight = jnp.where(lane == 0, 0.0, 0.5 * (fluid + rf))
            left = rp
        else:
            weight = 0.5 * (fluid + jnp.where(lane == 0, before[1], rf))
            left = jnp.where(lane == 0, before[0], rp)
        py = weight * (v[i, 1] - (pres - left))
        zy[i, 1] = py
        stores.append(copy(zy.at[i], proj_h.at[pl.ds(1, 2), :, pl.ds(i * ty, ty)], sem_zy.at[i]))
        stores[-1].start()
        op[i, :, 1] = (dz - py).reshape(nz, tz, ty)
        ry = pltpu.roll(py, ty - 1, 1)
        if i:
            op[i - 1, :, 1] += jnp.where(lane == ty - 1, ry, before[2]).reshape(nz, tz, ty)
        before = rp, rf, ry
    op[ny - 1, :, 1] += jnp.where(lane == ty - 1, 0.0, before[2]).reshape(nz, tz, ty)
    wait(stores)


def final_kernel(r, px_h, proj_in, proj_h, div_h, px, div, sem_x, sem_p, sem_d):
    del proj_in
    ny, nz, _, tz, ty = r.shape
    copy = pltpu.make_async_copy
    loads = [copy(px_h.at[i], px.at[i], sem_x.at[i]) for i in range(ny)]
    start(loads)
    stores = [copy(r.at[i, :, 0], proj_h.at[0, :, :, pl.ds(i * ty, ty)], sem_p.at[i]) for i in range(ny)]
    start(stores)
    loads[0].wait()
    for i in range(ny):
        if i + 1 < ny:
            loads[i + 1].wait()
        for j in range(nz):
            if j < nz - 1:
                after = px[i, j + 1]
            else:
                after = px[i + 1, 0] if i < ny - 1 else 0.0
            div[i, j] = r[i, j, 1] + (after - px[i, j])
        stores.append(copy(div.at[i], div_h.at[i], sem_d.at[i]))
        stores[-1].start()
    wait(stores)


def exchange(blocks):
    ny, nz = blocks.shape[:2]
    flat = blocks.reshape(ny * nz, *blocks.shape[2:])
    return lax.all_to_all(flat, BOTH, split_axis=0, concat_axis=0, tiled=True).reshape(blocks.shape)


def on_device(velocity, fluid, pressure):
    ny = lax.axis_size("py")
    nz = lax.axis_size("pz")
    _, depth, across = fluid.shape
    tz, ty = pressure.shape[1:]
    plane = depth * across * 4
    p4 = pressure.reshape(ny, nz, tz, ty)
    tiles = (ny, nz, tz, ty)
    sems = DMA((ny,))
    far = pltpu.HBM

    (packed,) = call(
        pack_kernel, [((ny, nz, 3, tz, ty), VMEM)],
        [(fluid.reshape(nz, tz, across), far), (velocity.reshape(3, nz, tz, across), far), (p4, far)],
        [sems, sems, DMA], 8, 3 * plane,
    )
    first = exchange(packed)
    op, partial, px = call(
        middle_kernel, [((ny, nz, 2, tz, ty), VMEM), ((3, depth, across), far), (tiles, far)],
        [(first, VMEM), (p4, far), (fluid.reshape(depth, across), far), (velocity.reshape(3, depth, across), far)],
        [VMEM(tiles, F32), VMEM((ny, depth, ty), F32), VMEM((ny, 2, depth, ty), F32), VMEM((ny, 2, depth, ty), F32),
         VMEM(tiles, F32)] + [sems] * 5, 32, 7 * plane,
    )
    second = exchange(op)
    projected, divergence = call(
        final_kernel, [((3, nz, tz, across), far), (tiles, far)],
        [(second, VMEM), (px, far), (partial.reshape(3, nz, tz, across), far)],
        [VMEM(tiles, F32)] * 2 + [sems] * 3, 16, 3 * plane,
        input_output_aliases={2: 0},
    )
    return projected.reshape(velocity.shape), divergence.reshape(pressure.shape)


def solution(mesh):
    placed = (P(None, BOTH, None, None), P(BOTH, None, None), P(None, "pz", "py"))
    return jax.shard_map(
        on_device,
        mesh=mesh,
        in_specs=placed,
        out_specs=(P(None, BOTH, None, None), P(None, "pz", "py")),
        check_vma=False,
    )
```

time: 138 us -> 98.7 us (0.72)
  waiting for transfers between devices: 88.2 us -> 0 us
  blocking collectives: 0 us -> 87.8 us
  starting transfers between devices: 35.5 us -> 0 us
  Pallas kernels: 0 us -> 9.93 us
  other arithmetic: 7.29 us -> 0 us
  local copies, waits for them, and re-layouts: 5.97 us -> 0 us
    all_to_all x0 -> x2, blocking collectives: none -> 87.8 us  [exchange(): lax.all_to_all(flat, BOTH, split_axis=0, concat_axis=0, tiled=True)]
    ppermute x3 -> x0, waiting for transfers between devices: 55.1 us -> none  [from_behind(): return lax.ppermute(shard, axis, pairs)]
    all_to_all x2 -> x0, waiting for transfers between devices: 33.1 us -> none  [the longest x1 16.8 us: on_device(): lax.all_to_all(blocks, ('py', 'pz'), split_axis=0, concat_axis=0, tiled=T...]
    all_to_all x2 -> x0, starting transfers between devices: 22.9 us -> none  [the longest x1 11.5 us: on_device(): lax.all_to_all(outgoing, ('py', 'pz'), split_axis=0, concat_axis=0, tiled...]
    ppermute x3 -> x0, starting transfers between devices: 12.6 us -> none  [from_behind(): return lax.ppermute(shard, axis, pairs)]
    pallas_call x0 -> x3, Pallas kernels: none -> 9.93 us  [call(): pl.pallas_call(kernel, out_shape=tuple((space(shape, F32) for shape, spac...]
    mul x1 -> x0, other arithmetic: 4.78 us -> none  [face_update(): weight * (component - (pressure - before_along(pressure, pressure_low, ax...]
    unnamed x8 -> x0, local copies, waits for them, and re-layouts: 3.43 us -> none
  transfers between devices with their start and end apart: 5 -> 0, of which waited for: 5 -> 0; matrix products, arithmetic and copies ran while one was open for 2% -> 0% of each run, Pallas kernels for 0% -> 0%
where the time goes in v1:
time: 98.7 us; the launch traced here: 98.4 us
  blocking collectives  87.8 us (89%)
  Pallas kernels  9.93 us (10%)
    all_to_all x2, blocking collectives, exchange(): lax.all_to_all(flat, BOTH, split_axis=0, concat_axis=0, tiled=True)  87.8 us
    pallas_call x3, Pallas kernels, call(): pl.pallas_call(kernel, out_shape=tuple((space(shape, F32) for shape, spac...  9.93 us

profile of v1, /device:TPU:1, one launch (start us, length us, event | category | flops | bytes accessed | tf_op | source)
XLA Modules:
  0.0 98.4 jit_solution(4651249218268347837)
XLA Ops:
  0.6 2.1 %shard_map.50 = f32[16,8,3,16,128]{4,3,2,1,0:T(8,128)S(1)} custom-call(f32[8,16,2048]{2,1,0:T(8,128)} %bitcast.20, f32[3,8,16,2048]{3,2,1,0:T(8,128)} %bitcast.18, f32[16,8,16,128]{3,2,1,0:T(8,128)} %bitcast.22), custom_call_target="tpu_custom_call" | custom-call | flops 3145728 | bytes 3145728 | tf_op jit(solution)/shard_map/pallas_call | solution.py:17
  2.7 52.8 %all_to_all.10 = f32[128,3,16,128]{3,2,1,0:T(8,128)S(1)} all-to-all(f32[128,3,16,128]{3,2,1,0:T(8,128)S(1)} %bitcast.15), channel_id=1, replica_groups=mesh['py'=16,'pz'=8] {'py','pz'}, dimensions={0} | all-to-all | bytes 6291456 | tf_op jit(solution)/shard_map/all_to_all | solution.py:131
  55.5 5.1 %shard_map.51 = (f32[16,8,2,16,128]{4,3,2,1,0:T(8,128)S(1)}, f32[3,128,2048]{2,1,0:T(8,128)}, f32[16,8,16,128]{3,2,1,0:T(8,128)}) custom-call(f32[16,8,3,16,128]{4,3,2,1,0:T(8,128)S(1)} %bitcast.14, f32[16,8,16,128]{3,2,1,0:T(8,128)} %bitcast.23, f32[128,2048]{1,0:T(8,128)} %bitcast.21, f32[3,128,2048]{2,1,0:T(8,128)} %bitcast.19), custom_call_target="tpu_custom_call" | custom-call | flops 7340032 | bytes 7340032 | tf_op jit(solution)/shard_map/pallas_call | solution.py:17
  60.7 35.0 %all_to_all.11 = f32[128,2,16,128]{3,2,1,0:T(8,128)S(1)} all-to-all(f32[128,2,16,128]{3,2,1,0:T(8,128)S(1)} %bitcast.17), channel_id=1, replica_groups=mesh['py'=16,'pz'=8] {'py','pz'}, dimensions={0} | all-to-all | bytes 4194304 | tf_op jit(solution)/shard_map/all_to_all | solution.py:131
  95.7 2.7 %shard_map.52 = (f32[3,8,16,2048]{3,2,1,0:T(8,128)}, f32[16,8,16,128]{3,2,1,0:T(8,128)}) custom-call(f32[16,8,2,16,128]{4,3,2,1,0:T(8,128)S(1)} %bitcast.16, f32[16,8,16,128]{3,2,1,0:T(8,128)} %get-tuple-element.8.px_h, f32[3,8,16,2048]{3,2,1,0:T(8,128)} %bitcast.24), custom_call_target="tpu_custom_call", output_to_operand_aliasing={{0}: (2, {})} | custom-call | flops 3145728 | bytes 3145728 | tf_op jit(solution)/shard_map/pallas_call | solution.py:17

commit v2 on v1

v2 whole, which is shorter than its diff:
```python
import jax
import jax.numpy as jnp
from jax import lax
from jax.experimental import pallas as pl
from jax.experimental.pallas import tpu as pltpu
from jax.sharding import PartitionSpec as P

ANY = pl.ANY
BOTH = ("py", "pz")
F32 = jnp.float32
HBM = pl.BlockSpec(memory_space=pltpu.HBM)
VMEM = pltpu.VMEM
DMA = pltpu.SemaphoreType.DMA


def call(kernel, outs, ins, scratch, mib, moved, **more):
    spec = {ANY: HBM, pltpu.HBM: HBM, None: pl.BlockSpec(memory_space=VMEM), VMEM: pl.BlockSpec(memory_space=VMEM)}
    return pl.pallas_call(
        kernel,
        out_shape=tuple((space or jax.ShapeDtypeStruct)(shape, F32) for shape, space in outs),
        in_specs=[spec[space] for _, space in ins],
        out_specs=tuple(spec[space] for _, space in outs),
        scratch_shapes=scratch,
        compiler_params=pltpu.CompilerParams(vmem_limit_bytes=mib * 1024 * 1024),
        cost_estimate=pl.CostEstimate(flops=moved, bytes_accessed=moved, transcendentals=0),
        **more,
    )(*(x if space in (None, ANY) else pltpu.with_memory_space_constraint(x, space) for x, space in ins))


def start(copies):
    for c in copies:
        c.start()


def wait(copies):
    for c in copies:
        c.wait()


def pack_kernel(f_h, v_h, p_h, out, p, wz, wy, f, v, sem_f, sem_v, sem_p):
    ny, nz, _, tz, ty = out.shape
    depth = nz * tz
    copy = pltpu.make_async_copy
    part = nz // 4
    rows = [pl.ds(k * part * tz, part * tz) for k in range(4)]
    loads_f = [copy(f_h.at[k], f.at[k], sem_f.at[i]) for i, k in enumerate(rows)]
    loads_v = [copy(v_h.at[0, k], v.at[k], sem_v.at[i]) for i, k in enumerate(rows)]
    load_p = copy(p_h, p, sem_p)
    start(loads_f)
    load_p.start()
    start(loads_v)
    row = lax.broadcasted_iota(jnp.int32, (depth, ty), 0)
    lane = lax.broadcasted_iota(jnp.int32, (depth, ty), 1)
    before = None
    wait(loads_f)
    for i in range(ny):
        fluid = f[:, pl.ds(i * ty, ty)]
        out[i, :, 0] = fluid.reshape(nz, tz, ty)
        wz[i] = jnp.where(row == 0, 0.0, 0.5 * (fluid + pltpu.roll(fluid, 1, 0)))
        turned = pltpu.roll(fluid, 1, 1)
        if i:
            wy[i] = 0.5 * (fluid + jnp.where(lane == 0, before, turned))
        else:
            wy[i] = jnp.where(lane == 0, 0.0, 0.5 * (fluid + turned))
        before = turned
    load_p.wait()
    for i in range(ny):
        out[i, :, 2] = p[i]
    for k in range(4):
        loads_v[k].wait()
        for i in range(ny):
            out[i, k * part : (k + 1) * part, 1] = v[rows[k], pl.ds(i * ty, ty)].reshape(part, tz, ty)


def middle_kernel(r, p, wz, wy, v, op, proj_h, px, faces, sems):
    ny, nz, _, tz, ty = r.shape
    depth = nz * tz
    row = lax.broadcasted_iota(jnp.int32, (depth, ty), 0)
    lane = lax.broadcasted_iota(jnp.int32, (depth, ty), 1)
    before = None
    stores = []
    for i in range(ny):
        for j in range(nz):
            if i == 0 and j == 0:
                op[0, 0, 0] = px[0, 0] = jnp.zeros((tz, ty), F32)
                continue
            a, b = (i, j - 1) if j else (i - 1, nz - 1)
            weight = 0.5 * (r[i, j, 0] + r[a, b, 0])
            op[i, j, 0] = px[i, j] = weight * (r[i, j, 1] - (p[i, j] - p[a, b]))
        cols = pl.ds(i * ty, ty)
        pres = r[i, :, 2].reshape(depth, ty)
        pz = wz[i] * (v[1, :, cols] - (pres - pltpu.roll(pres, 1, 0)))
        faces[0, :, cols] = pz
        dz = jnp.where(row == depth - 1, 0.0, pltpu.roll(pz, depth - 1, 0)) - pz
        rp = pltpu.roll(pres, 1, 1)
        left = jnp.where(lane == 0, before[0], rp) if i else rp
        py = wy[i] * (v[2, :, cols] - (pres - left))
        faces[1, :, cols] = py
        op[i, :, 1] = (dz - py).reshape(nz, tz, ty)
        if i % 4 == 3:
            done = pl.ds((i - 3) * ty, 4 * ty)
            stores.append(pltpu.make_async_copy(faces.at[:, :, done], proj_h.at[pl.ds(1, 2), :, done], sems.at[i // 4]))
            stores[-1].start()
        ry = pltpu.roll(py, ty - 1, 1)
        if i:
            op[i - 1, :, 1] += jnp.where(lane == ty - 1, ry, before[1]).reshape(nz, tz, ty)
        before = rp, ry
    op[ny - 1, :, 1] += jnp.where(lane == ty - 1, 0.0, before[1]).reshape(nz, tz, ty)
    wait(stores)


def final_kernel(r, px, faces, proj_h, div_h, first, div, sem_p, sem_d):
    del faces
    ny, nz, _, tz, ty = r.shape
    copy = pltpu.make_async_copy
    part = nz // 4
    stores = []
    for k in range(4):
        for j in range(k * part, (k + 1) * part):
            for i in range(ny):
                first[j, :, i * ty : (i + 1) * ty] = r[i, j, 0]
        rows = pl.ds(k * part, part)
        stores.append(copy(first.at[rows], proj_h.at[0, rows], sem_p.at[k]))
        stores[-1].start()
    quarter = ny // 4
    for k in range(4):
        for i in range(k * quarter, (k + 1) * quarter):
            for j in range(nz):
                if j < nz - 1:
                    after = px[i, j + 1]
                else:
                    after = px[i + 1, 0] if i < ny - 1 else 0.0
                div[i, j] = r[i, j, 1] + (after - px[i, j])
        rows = pl.ds(k * quarter, quarter)
        stores.append(copy(div.at[rows], div_h.at[rows], sem_d.at[k]))
        stores[-1].start()
    wait(stores)


def exchange(blocks):
    ny, nz = blocks.shape[:2]
    flat = blocks.reshape(ny * nz, *blocks.shape[2:])
    return lax.all_to_all(flat, BOTH, split_axis=0, concat_axis=0, tiled=True).reshape(blocks.shape)


def on_device(velocity, fluid, pressure):
    ny = lax.axis_size("py")
    nz = lax.axis_size("pz")
    _, depth, across = fluid.shape
    tz, ty = pressure.shape[1:]
    plane = depth * across * 4
    p4 = pressure.reshape(ny, nz, tz, ty)
    tiles = (ny, nz, tz, ty)
    sems = DMA((ny,))
    far = pltpu.HBM

    slab = (ny, depth, ty)
    packed, p_near, wz, wy = call(
        pack_kernel, [((ny, nz, 3, tz, ty), VMEM), (tiles, VMEM), (slab, VMEM), (slab, VMEM)],
        [(fluid.reshape(depth, across), far), (velocity.reshape(3, depth, across), far), (p4, far)],
        [VMEM((depth, across), F32)] * 2 + [DMA((4,)), DMA((4,)), DMA], 24, 9 * plane,
    )
    first = exchange(packed)
    op, faces, px = call(
        middle_kernel, [((ny, nz, 2, tz, ty), VMEM), ((3, depth, across), far), (tiles, VMEM)],
        [(first, VMEM), (p_near, VMEM), (wz, VMEM), (wy, VMEM), (velocity.reshape(3, depth, across), None)],
        [VMEM((2, depth, across), F32), DMA((4,))], 24, 7 * plane,
    )
    second = exchange(op)
    projected, divergence = call(
        final_kernel, [((3, nz, tz, across), far), (tiles, far)],
        [(second, VMEM), (px, VMEM), (faces.reshape(3, nz, tz, across), far)],
        [VMEM((nz, tz, across), F32), VMEM(tiles, F32), DMA((4,)), DMA((4,))], 16, 3 * plane,
        input_output_aliases={2: 0},
    )
    return projected.reshape(velocity.shape), divergence.reshape(pressure.shape)


def solution(mesh):
    placed = (P(None, BOTH, None, None), P(BOTH, None, None), P(None, "pz", "py"))
    return jax.shard_map(
        on_device,
        mesh=mesh,
        in_specs=placed,
        out_specs=(P(None, BOTH, None, None), P(None, "pz", "py")),
        check_vma=False,
    )
```

time: 98.7 us -> 94.2 us (0.954)
  Pallas kernels: 9.93 us -> 5.6 us
    pallas_call x3, Pallas kernels: 9.93 us -> 5.6 us  [call(): pl.pallas_call(kernel, out_shape=tuple(((space or jax.ShapeDtypeStruct)(s...]
where the time goes in v2:
time: 94.2 us; the launch traced here: 94.1 us
  blocking collectives  87.8 us (93%)
  Pallas kernels  5.6 us (6%)
    all_to_all x2, blocking collectives, exchange(): lax.all_to_all(flat, BOTH, split_axis=0, concat_axis=0, tiled=True)  87.8 us
    pallas_call x3, Pallas kernels, call(): pl.pallas_call(kernel, out_shape=tuple(((space or jax.ShapeDtypeStruct)(s...  5.6 us

profile of v2, /device:TPU:1, one launch (start us, length us, event | category | flops | bytes accessed | tf_op | source)
XLA Modules:
  0.0 94.1 jit_solution(17935128426147577337)
XLA Ops:
  0.6 2.0 %shard_map.50 = (f32[16,8,3,16,128]{4,3,2,1,0:T(8,128)S(1)}, f32[16,8,16,128]{3,2,1,0:T(8,128)S(1)}, f32[16,128,128]{2,1,0:T(8,128)S(1)}, f32[16,128,128]{2,1,0:T(8,128)S(1)}) custom-call(f32[128,2048]{1,0:T(8,128)} %bitcast.20, f32[3,128,2048]{2,1,0:T(8,128)} %bitcast.12, f32[16,8,16,128]{3,2,1,0:T(8,128)} %bitcast.21), custom_call_target="tpu_custom_call" | custom-call | flops 9437184 | bytes 9437184 | tf_op jit(solution)/shard_map/pallas_call | solution.py:18
  2.6 0.0 copy-start
  2.7 52.8 %all_to_all.10 = f32[128,3,16,128]{3,2,1,0:T(8,128)S(1)} all-to-all(f32[128,3,16,128]{3,2,1,0:T(8,128)S(1)} %bitcast.16), channel_id=1, replica_groups=mesh['py'=16,'pz'=8] {'py','pz'}, dimensions={0} | all-to-all | bytes 6291456 | tf_op jit(solution)/shard_map/all_to_all | solution.py:143
  55.4 0.0 copy-done
  55.5 2.2 %shard_map.51 = (f32[16,8,2,16,128]{4,3,2,1,0:T(8,128)S(1)}, f32[3,128,2048]{2,1,0:T(8,128)}, f32[16,8,16,128]{3,2,1,0:T(8,128)S(1)}) custom-call(f32[16,8,3,16,128]{4,3,2,1,0:T(8,128)S(1)} %bitcast.14, f32[16,8,16,128]{3,2,1,0:T(8,128)S(1)} %get-tuple-element.12.p, f32[16,128,128]{2,1,0:T(8,128)S(1)} %get-tuple-element.13.wz, ...), custom_call_target="tpu_custom_call" | custom-call | flops 7340032 | bytes 7340032 | tf_op jit(solution)/shard_map/pallas_call | solution.py:18
  57.7 35.0 %all_to_all.11 = f32[128,2,16,128]{3,2,1,0:T(8,128)S(1)} all-to-all(f32[128,2,16,128]{3,2,1,0:T(8,128)S(1)} %bitcast.17), channel_id=1, replica_groups=mesh['py'=16,'pz'=8] {'py','pz'}, dimensions={0} | all-to-all | bytes 4194304 | tf_op jit(solution)/shard_map/all_to_all | solution.py:143
  92.7 1.4 %shard_map.52 = (f32[3,8,16,2048]{3,2,1,0:T(8,128)}, f32[16,8,16,128]{3,2,1,0:T(8,128)}) custom-call(f32[16,8,2,16,128]{4,3,2,1,0:T(8,128)S(1)} %bitcast.15, f32[16,8,16,128]{3,2,1,0:T(8,128)S(1)} %get-tuple-element.16.px, f32[3,8,16,2048]{3,2,1,0:T(8,128)} %bitcast.18), custom_call_target="tpu_custom_call", output_to_operand_aliasing={{0}: (2, {})} | custom-call | flops 3145728 | bytes 3145728 | tf_op jit(solution)/shard_map/pallas_call | solution.py:18
Async XLA Ops:
  2.6 52.8 %copy-start = (f32[3,1,128,2048]{3,2,1,0:T(8,128)S(1)}, f32[3,1,128,2048]{3,2,1,0:T(8,128)}, u32[]{:S(2)}) copy-start(f32[3,1,128,2048]{3,2,1,0:T(8,128)} %param.3) | copy-start | bytes 9437188

commit v3 on v2

--- a/solution.py
+++ b/solution.py
@@ -39,30 +39,37 @@
 
 def pack_kernel(f_h, v_h, p_h, out, p, wz, wy, f, v, sem_f, sem_v, sem_p):
     ny, nz, _, tz, ty = out.shape
-    depth = nz * tz
     copy = pltpu.make_async_copy
     part = nz // 4
-    rows = [pl.ds(k * part * tz, part * tz) for k in range(4)]
+    high = part * tz
+    rows = [pl.ds(k * high, high) for k in range(4)]
     loads_f = [copy(f_h.at[k], f.at[k], sem_f.at[i]) for i, k in enumerate(rows)]
     loads_v = [copy(v_h.at[0, k], v.at[k], sem_v.at[i]) for i, k in enumerate(rows)]
     load_p = copy(p_h, p, sem_p)
     start(loads_f)
     load_p.start()
     start(loads_v)
-    row = lax.broadcasted_iota(jnp.int32, (depth, ty), 0)
-    lane = lax.broadcasted_iota(jnp.int32, (depth, ty), 1)
-    before = None
-    wait(loads_f)
-    for i in range(ny):
-        fluid = f[:, pl.ds(i * ty, ty)]
-        out[i, :, 0] = fluid.reshape(nz, tz, ty)
-        wz[i] = jnp.where(row == 0, 0.0, 0.5 * (fluid + pltpu.roll(fluid, 1, 0)))
-        turned = pltpu.roll(fluid, 1, 1)
-        if i:
-            wy[i] = 0.5 * (fluid + jnp.where(lane == 0, before, turned))
-        else:
-            wy[i] = jnp.where(lane == 0, 0.0, 0.5 * (fluid + turned))
-        before = turned
+    lane = lax.broadcasted_iota(jnp.int32, (high, ty), 1)
+    for k in range(4):
+        loads_f[k].wait()
+        before = None
+        for i in range(ny):
+            cols = pl.ds(i * ty, ty)
+            if k:
+                tall = 0.5 * f[pl.ds(k * high - 8, high + 8), cols]
+                half, above = tall[8:], pltpu.roll(tall, 1, 0)[8:]
+                wz[i, rows[k]] = half + above
+            else:
+                half = 0.5 * f[rows[k], cols]
+                row = lax.broadcasted_iota(jnp.int32, (high, ty), 0)
+                wz[i, rows[k]] = jnp.where(row == 0, 0.0, half + pltpu.roll(half, 1, 0))
+            out[i, k * part : (k + 1) * part, 0] = half.reshape(part, tz, ty)
+            turned = pltpu.roll(half, 1, 1)
+            if i:
+                wy[i, rows[k]] = half + jnp.where(lane == 0, before, turned)
+            else:
+                wy[i, rows[k]] = jnp.where(lane == 0, 0.0, half + turned)
+            before = turned
     load_p.wait()
     for i in range(ny):
         out[i, :, 2] = p[i]
@@ -72,49 +79,50 @@
             out[i, k * part : (k + 1) * part, 1] = v[rows[k], pl.ds(i * ty, ty)].reshape(part, tz, ty)
 
 
-def middle_kernel(r, p, wz, wy, v, op, proj_h, px, faces, sems):
+def middle_kernel(r, p, wz, wy, v, op, proj_h, faces, sems):
     ny, nz, _, tz, ty = r.shape
     depth = nz * tz
-    row = lax.broadcasted_iota(jnp.int32, (depth, ty), 0)
     lane = lax.broadcasted_iota(jnp.int32, (depth, ty), 1)
     before = None
     stores = []
     for i in range(ny):
-        for j in range(nz):
-            if i == 0 and j == 0:
-                op[0, 0, 0] = px[0, 0] = jnp.zeros((tz, ty), F32)
-                continue
-            a, b = (i, j - 1) if j else (i - 1, nz - 1)
-            weight = 0.5 * (r[i, j, 0] + r[a, b, 0])
-            op[i, j, 0] = px[i, j] = weight * (r[i, j, 1] - (p[i, j] - p[a, b]))
         cols = pl.ds(i * ty, ty)
         pres = r[i, :, 2].reshape(depth, ty)
         pz = wz[i] * (v[1, :, cols] - (pres - pltpu.roll(pres, 1, 0)))
         faces[0, :, cols] = pz
-        dz = jnp.where(row == depth - 1, 0.0, pltpu.roll(pz, depth - 1, 0)) - pz
+        dz = pltpu.roll(pz, depth - 1, 0) - pz
         rp = pltpu.roll(pres, 1, 1)
         left = jnp.where(lane == 0, before[0], rp) if i else rp
         py = wy[i] * (v[2, :, cols] - (pres - left))
         faces[1, :, cols] = py
-        op[i, :, 1] = (dz - py).reshape(nz, tz, ty)
-        if i % 4 == 3:
+        if i % 4 == 3 and i < ny - 1:
             done = pl.ds((i - 3) * ty, 4 * ty)
             stores.append(pltpu.make_async_copy(faces.at[:, :, done], proj_h.at[pl.ds(1, 2), :, done], sems.at[i // 4]))
             stores[-1].start()
         ry = pltpu.roll(py, ty - 1, 1)
         if i:
-            op[i - 1, :, 1] += jnp.where(lane == ty - 1, ry, before[1]).reshape(nz, tz, ty)
-        before = rp, ry
-    op[ny - 1, :, 1] += jnp.where(lane == ty - 1, 0.0, before[1]).reshape(nz, tz, ty)
+            op[i - 1, :, 1] = (before[2] + jnp.where(lane == ty - 1, ry, before[1])).reshape(nz, tz, ty)
+        before = rp, ry, dz - py
+    op[ny - 1, :, 1] = (before[2] + jnp.where(lane == ty - 1, 0.0, before[1])).reshape(nz, tz, ty)
+    for i in range(ny):
+        for j in range(nz):
+            if i == 0 and j == 0:
+                op[0, 0, 0] = jnp.zeros((tz, ty), F32)
+                continue
+            a, b = (i, j - 1) if j else (i - 1, nz - 1)
+            weight = r[i, j, 0] + r[a, b, 0]
+            op[i, j, 0] = weight * (r[i, j, 1] - (p[i, j] - p[a, b]))
     wait(stores)
 
 
-def final_kernel(r, px, faces, proj_h, div_h, first, div, sem_p, sem_d):
-    del faces
+def final_kernel(r, op, faces, partial, proj_h, div_h, first, div, sem_p, sem_d, sem_f):
+    del partial
     ny, nz, _, tz, ty = r.shape
     copy = pltpu.make_async_copy
     part = nz // 4
-    stores = []
+    late = pl.ds((ny - 4) * ty, 4 * ty)
+    stores = [copy(faces.at[:, :, :, late], proj_h.at[pl.ds(1, 2), :, :, late], sem_f)]
+    start(stores)
     for k in range(4):
         for j in range(k * part, (k + 1) * part):
             for i in range(ny):
@@ -127,10 +135,10 @@
         for i in range(k * quarter, (k + 1) * quarter):
             for j in range(nz):
                 if j < nz - 1:
-                    after = px[i, j + 1]
+                    after = op[i, j + 1, 0]
                 else:
-                    after = px[i + 1, 0] if i < ny - 1 else 0.0
-                div[i, j] = r[i, j, 1] + (after - px[i, j])
+                    after = op[i + 1, 0, 0] if i < ny - 1 else 0.0
+                div[i, j] = r[i, j, 1] + (after - op[i, j, 0])
         rows = pl.ds(k * quarter, quarter)
         stores.append(copy(div.at[rows], div_h.at[rows], sem_d.at[k]))
         stores[-1].start()
@@ -161,17 +169,17 @@
         [VMEM((depth, across), F32)] * 2 + [DMA((4,)), DMA((4,)), DMA], 24, 9 * plane,
     )
     first = exchange(packed)
-    op, faces, px = call(
-        middle_kernel, [((ny, nz, 2, tz, ty), VMEM), ((3, depth, across), far), (tiles, VMEM)],
+    op, partial, faces = call(
+        middle_kernel, [((ny, nz, 2, tz, ty), VMEM), ((3, depth, across), far), ((2, depth, across), VMEM)],
         [(first, VMEM), (p_near, VMEM), (wz, VMEM), (wy, VMEM), (velocity.reshape(3, depth, across), None)],
-        [VMEM((2, depth, across), F32), DMA((4,))], 24, 7 * plane,
+        [DMA((4,))], 24, 7 * plane,
     )
     second = exchange(op)
     projected, divergence = call(
         final_kernel, [((3, nz, tz, across), far), (tiles, far)],
-        [(second, VMEM), (px, VMEM), (faces.reshape(3, nz, tz, across), far)],
-        [VMEM((nz, tz, across), F32), VMEM(tiles, F32), DMA((4,)), DMA((4,))], 16, 3 * plane,
-        input_output_aliases={2: 0},
+        [(second, VMEM), (op, VMEM), (faces.reshape(2, nz, tz, across), VMEM), (partial.reshape(3, nz, tz, across), far)],
+        [VMEM((nz, tz, across), F32), VMEM(tiles, F32), DMA((4,)), DMA((4,)), DMA], 16, 3 * plane,
+        input_output_aliases={3: 0},
     )
     return projected.reshape(velocity.shape), divergence.reshape(pressure.shape)
 

time: 94.2 us -> 94 us (level)
  no operation moved by 1% of the time
where the time goes in v3:
time: 94 us; the launch traced here: 93.9 us
  blocking collectives  87.8 us (93%)
  Pallas kernels  5.4 us (6%)
    all_to_all x2, blocking collectives, exchange(): lax.all_to_all(flat, BOTH, split_axis=0, concat_axis=0, tiled=True)  87.8 us
    pallas_call x3, Pallas kernels, call(): pl.pallas_call(kernel, out_shape=tuple(((space or jax.ShapeDtypeStruct)(s...  5.4 us

profile of v3, /device:TPU:1, one launch (start us, length us, event | category | flops | bytes accessed | tf_op | source)
XLA Modules:
  0.0 93.9 jit_solution(7238565576906782796)
XLA Ops:
  0.6 2.0 %shard_map.50 = (f32[16,8,3,16,128]{4,3,2,1,0:T(8,128)S(1)}, f32[16,8,16,128]{3,2,1,0:T(8,128)S(1)}, f32[16,128,128]{2,1,0:T(8,128)S(1)}, f32[16,128,128]{2,1,0:T(8,128)S(1)}) custom-call(f32[128,2048]{1,0:T(8,128)} %bitcast.22, f32[3,128,2048]{2,1,0:T(8,128)} %bitcast.13, f32[16,8,16,128]{3,2,1,0:T(8,128)} %bitcast.23), custom_call_target="tpu_custom_call" | custom-call | flops 9437184 | bytes 9437184 | tf_op jit(solution)/shard_map/pallas_call | solution.py:18
  2.6 0.0 copy-start
  2.7 52.8 %all_to_all.10 = f32[128,3,16,128]{3,2,1,0:T(8,128)S(1)} all-to-all(f32[128,3,16,128]{3,2,1,0:T(8,128)S(1)} %bitcast.18), channel_id=1, replica_groups=mesh['py'=16,'pz'=8] {'py','pz'}, dimensions={0} | all-to-all | bytes 6291456 | tf_op jit(solution)/shard_map/all_to_all | solution.py:151
  55.4 0.0 copy-done
  55.5 1.8 %shard_map.51 = (f32[16,8,2,16,128]{4,3,2,1,0:T(8,128)S(1)}, f32[3,128,2048]{2,1,0:T(8,128)}, f32[2,128,2048]{2,1,0:T(8,128)S(1)}) custom-call(f32[16,8,3,16,128]{4,3,2,1,0:T(8,128)S(1)} %bitcast.15, f32[16,8,16,128]{3,2,1,0:T(8,128)S(1)} %get-tuple-element.12.p, f32[16,128,128]{2,1,0:T(8,128)S(1)} %get-tuple-element.13.wz, ...), custom_call_target="tpu_custom_call" | custom-call | flops 7340032 | bytes 7340032 | tf_op jit(solution)/shard_map/pallas_call | solution.py:18
  57.3 35.0 %all_to_all.11 = f32[128,2,16,128]{3,2,1,0:T(8,128)S(1)} all-to-all(f32[128,2,16,128]{3,2,1,0:T(8,128)S(1)} %bitcast.16), channel_id=1, replica_groups=mesh['py'=16,'pz'=8] {'py','pz'}, dimensions={0} | all-to-all | bytes 4194304 | tf_op jit(solution)/shard_map/all_to_all | solution.py:151
  92.3 1.6 %shard_map.52 = (f32[3,8,16,2048]{3,2,1,0:T(8,128)}, f32[16,8,16,128]{3,2,1,0:T(8,128)}) custom-call(f32[16,8,2,16,128]{4,3,2,1,0:T(8,128)S(1)} %bitcast.17, f32[16,8,2,16,128]{4,3,2,1,0:T(8,128)S(1)} %get-tuple-element.15.op, f32[2,8,16,2048]{3,2,1,0:T(8,128)S(1)} %bitcast.19, f32[3,8,16,2048]{3,2,1,0:T(8,128)} %bitcast.20), custom_call_target="tpu_custom_call", output_to_operand_aliasing={{0}: (3, {})} | custom-call | flops 3145728 | bytes 3145728 | tf_op jit(solution)/shard_map/pallas_call | solution.py:18
Async XLA Ops:
  2.6 52.8 %copy-start = (f32[3,1,128,2048]{3,2,1,0:T(8,128)S(1)}, f32[3,1,128,2048]{3,2,1,0:T(8,128)}, u32[]{:S(2)}) copy-start(f32[3,1,128,2048]{3,2,1,0:T(8,128)} %param.3) | copy-start | bytes 9437188

commit v4 on v3

--- a/solution.py
+++ b/solution.py
@@ -37,15 +37,15 @@
         c.wait()
 
 
-def pack_kernel(f_h, v_h, p_h, out, p, wz, wy, f, v, sem_f, sem_v, sem_p):
+def pack_kernel(f_h, v_h, p_h, out, wz, wy, f, sem_f, sem_v, sem_p):
     ny, nz, _, tz, ty = out.shape
     copy = pltpu.make_async_copy
     part = nz // 4
     high = part * tz
     rows = [pl.ds(k * high, high) for k in range(4)]
     loads_f = [copy(f_h.at[k], f.at[k], sem_f.at[i]) for i, k in enumerate(rows)]
-    loads_v = [copy(v_h.at[0, k], v.at[k], sem_v.at[i]) for i, k in enumerate(rows)]
-    load_p = copy(p_h, p, sem_p)
+    load_p = copy(p_h, out.at[:, :, 2], sem_p)
+    loads_v = [copy(v_h.at[0, :, :, pl.ds(i * ty, ty)], out.at[i, :, 1], sem_v.at[i]) for i in range(ny)]
     start(loads_f)
     load_p.start()
     start(loads_v)
@@ -71,12 +71,7 @@
                 wy[i, rows[k]] = jnp.where(lane == 0, 0.0, half + turned)
             before = turned
     load_p.wait()
-    for i in range(ny):
-        out[i, :, 2] = p[i]
-    for k in range(4):
-        loads_v[k].wait()
-        for i in range(ny):
-            out[i, k * part : (k + 1) * part, 1] = v[rows[k], pl.ds(i * ty, ty)].reshape(part, tz, ty)
+    wait(loads_v)
 
 
 def middle_kernel(r, p, wz, wy, v, op, proj_h, faces, sems):
@@ -86,6 +81,13 @@
     before = None
     stores = []
     for i in range(ny):
+        for j in range(nz):
+            if i == 0 and j == 0:
+                op[0, 0, 0] = jnp.zeros((tz, ty), F32)
+                continue
+            a, b = (i, j - 1) if j else (i - 1, nz - 1)
+            weight = r[i, j, 0] + r[a, b, 0]
+            op[i, j, 0] = weight * (r[i, j, 1] - (p[i, j] - p[a, b]))
         cols = pl.ds(i * ty, ty)
         pres = r[i, :, 2].reshape(depth, ty)
         pz = wz[i] * (v[1, :, cols] - (pres - pltpu.roll(pres, 1, 0)))
@@ -104,14 +106,6 @@
             op[i - 1, :, 1] = (before[2] + jnp.where(lane == ty - 1, ry, before[1])).reshape(nz, tz, ty)
         before = rp, ry, dz - py
     op[ny - 1, :, 1] = (before[2] + jnp.where(lane == ty - 1, 0.0, before[1])).reshape(nz, tz, ty)
-    for i in range(ny):
-        for j in range(nz):
-            if i == 0 and j == 0:
-                op[0, 0, 0] = jnp.zeros((tz, ty), F32)
-                continue
-            a, b = (i, j - 1) if j else (i - 1, nz - 1)
-            weight = r[i, j, 0] + r[a, b, 0]
-            op[i, j, 0] = weight * (r[i, j, 1] - (p[i, j] - p[a, b]))
     wait(stores)
 
 
@@ -163,15 +157,15 @@
     far = pltpu.HBM
 
     slab = (ny, depth, ty)
-    packed, p_near, wz, wy = call(
-        pack_kernel, [((ny, nz, 3, tz, ty), VMEM), (tiles, VMEM), (slab, VMEM), (slab, VMEM)],
-        [(fluid.reshape(depth, across), far), (velocity.reshape(3, depth, across), far), (p4, far)],
-        [VMEM((depth, across), F32)] * 2 + [DMA((4,)), DMA((4,)), DMA], 24, 9 * plane,
+    packed, wz, wy = call(
+        pack_kernel, [((ny, nz, 3, tz, ty), VMEM), (slab, VMEM), (slab, VMEM)],
+        [(fluid.reshape(depth, across), far), (velocity.reshape(3, nz, tz, across), far), (p4, far)],
+        [VMEM((depth, across), F32), DMA((4,)), sems, DMA], 24, 9 * plane,
     )
     first = exchange(packed)
     op, partial, faces = call(
         middle_kernel, [((ny, nz, 2, tz, ty), VMEM), ((3, depth, across), far), ((2, depth, across), VMEM)],
-        [(first, VMEM), (p_near, VMEM), (wz, VMEM), (wy, VMEM), (velocity.reshape(3, depth, across), None)],
+        [(first, VMEM), (p4, None), (wz, VMEM), (wy, VMEM), (velocity.reshape(3, depth, across), None)],
         [DMA((4,))], 24, 7 * plane,
     )
     second = exchange(op)

time: 94 us -> 94 us (level)
  no operation moved by 1% of the time
where the time goes in v4:
time: 94 us; the launch traced here: 93.8 us
  blocking collectives  87.8 us (93%)
  Pallas kernels  5.37 us (6%)
    all_to_all x2, blocking collectives, exchange(): lax.all_to_all(flat, BOTH, split_axis=0, concat_axis=0, tiled=True)  87.8 us
    pallas_call x3, Pallas kernels, call(): pl.pallas_call(kernel, out_shape=tuple(((space or jax.ShapeDtypeStruct)(s...  5.37 us

profile of v4, /device:TPU:1, one launch (start us, length us, event | category | flops | bytes accessed | tf_op | source)
XLA Modules:
  0.0 93.8 jit_solution(12843447837502075010)
XLA Ops:
  0.6 2.0 %shard_map.50 = (f32[16,8,3,16,128]{4,3,2,1,0:T(8,128)S(1)}, f32[16,128,128]{2,1,0:T(8,128)S(1)}, f32[16,128,128]{2,1,0:T(8,128)S(1)}) custom-call(f32[128,2048]{1,0:T(8,128)} %bitcast.25, f32[3,8,16,2048]{3,2,1,0:T(8,128)} %bitcast.14, f32[16,8,16,128]{3,2,1,0:T(8,128)} %bitcast.19), custom_call_target="tpu_custom_call" | custom-call | flops 9437184 | bytes 9437184 | tf_op jit(solution)/shard_map/pallas_call | solution.py:18
  2.6 0.0 copy-start
  2.6 0.0 copy-start.1
  2.6 52.8 %all_to_all.10 = f32[128,3,16,128]{3,2,1,0:T(8,128)S(1)} all-to-all(f32[128,3,16,128]{3,2,1,0:T(8,128)S(1)} %bitcast.21), channel_id=1, replica_groups=mesh['py'=16,'pz'=8] {'py','pz'}, dimensions={0} | all-to-all | bytes 6291456 | tf_op jit(solution)/shard_map/all_to_all | solution.py:145
  55.4 0.0 copy-done
  55.4 0.0 copy-done.1
  55.4 1.8 %shard_map.51 = (f32[16,8,2,16,128]{4,3,2,1,0:T(8,128)S(1)}, f32[3,128,2048]{2,1,0:T(8,128)}, f32[2,128,2048]{2,1,0:T(8,128)S(1)}) custom-call(f32[16,8,3,16,128]{4,3,2,1,0:T(8,128)S(1)} %bitcast.16, f32[16,8,16,128]{3,2,1,0:T(8,128)S(1)} %bitcast.20, f32[16,128,128]{2,1,0:T(8,128)S(1)} %get-tuple-element.11.wz, f32[16,128,128]{2,1,0:T(8,128)S(1)} %get-tuple-element.12.wy, ...), custom_call_target="tpu_custom_call" | custom-call | flops 7340032 | bytes 7340032 | tf_op jit(solution)/shard_map/pallas_call | solution.py:18
  57.3 35.0 %all_to_all.11 = f32[128,2,16,128]{3,2,1,0:T(8,128)S(1)} all-to-all(f32[128,2,16,128]{3,2,1,0:T(8,128)S(1)} %bitcast.17), channel_id=1, replica_groups=mesh['py'=16,'pz'=8] {'py','pz'}, dimensions={0} | all-to-all | bytes 4194304 | tf_op jit(solution)/shard_map/all_to_all | solution.py:145
  92.3 1.6 %shard_map.52 = (f32[3,8,16,2048]{3,2,1,0:T(8,128)}, f32[16,8,16,128]{3,2,1,0:T(8,128)}) custom-call(f32[16,8,2,16,128]{4,3,2,1,0:T(8,128)S(1)} %bitcast.18, f32[16,8,2,16,128]{4,3,2,1,0:T(8,128)S(1)} %get-tuple-element.13.op, f32[2,8,16,2048]{3,2,1,0:T(8,128)S(1)} %bitcast.22, f32[3,8,16,2048]{3,2,1,0:T(8,128)} %bitcast.23), custom_call_target="tpu_custom_call", output_to_operand_aliasing={{0}: (3, {})} | custom-call | flops 3145728 | bytes 3145728 | tf_op jit(solution)/shard_map/pallas_call | solution.py:18
Async XLA Ops:
  2.6 52.8 %copy-start = (f32[3,1,128,2048]{3,2,1,0:T(8,128)S(1)}, f32[3,1,128,2048]{3,2,1,0:T(8,128)}, u32[]{:S(2)}) copy-start(f32[3,1,128,2048]{3,2,1,0:T(8,128)} %param.3) | copy-start | bytes 9437188
  2.6 52.8 %copy-start.1 = (f32[128,16,128]{2,1,0:T(8,128)S(1)}, f32[128,16,128]{2,1,0:T(8,128)}, u32[]{:S(2)}) copy-start(f32[128,16,128]{2,1,0:T(8,128)} %param.5) | copy-start | bytes 3145732

commit v5 on v4

--- a/solution.py
+++ b/solution.py
@@ -97,7 +97,7 @@
         left = jnp.where(lane == 0, before[0], rp) if i else rp
         py = wy[i] * (v[2, :, cols] - (pres - left))
         faces[1, :, cols] = py
-        if i % 4 == 3 and i < ny - 1:
+        if i % 4 == 3 and i < ny // 2:
             done = pl.ds((i - 3) * ty, 4 * ty)
             stores.append(pltpu.make_async_copy(faces.at[:, :, done], proj_h.at[pl.ds(1, 2), :, done], sems.at[i // 4]))
             stores[-1].start()
@@ -114,7 +114,7 @@
     ny, nz, _, tz, ty = r.shape
     copy = pltpu.make_async_copy
     part = nz // 4
-    late = pl.ds((ny - 4) * ty, 4 * ty)
+    late = pl.ds(ny // 2 * ty, ny // 2 * ty)
     stores = [copy(faces.at[:, :, :, late], proj_h.at[pl.ds(1, 2), :, :, late], sem_f)]
     start(stores)
     for k in range(4):

time: 94 us -> 93.8 us (level)
  no operation moved by 1% of the time
where the time goes in v5:
time: 93.8 us; the launch traced here: 93.7 us
  blocking collectives  87.8 us (94%)
  Pallas kernels  5.18 us (6%)
    all_to_all x2, blocking collectives, exchange(): lax.all_to_all(flat, BOTH, split_axis=0, concat_axis=0, tiled=True)  87.8 us
    pallas_call x3, Pallas kernels, call(): pl.pallas_call(kernel, out_shape=tuple(((space or jax.ShapeDtypeStruct)(s...  5.18 us

profile of v5, /device:TPU:1, one launch (start us, length us, event | category | flops | bytes accessed | tf_op | source)
XLA Modules:
  0.0 93.7 jit_solution(5711417861264259243)
XLA Ops:
  0.6 2.0 %shard_map.50 = (f32[16,8,3,16,128]{4,3,2,1,0:T(8,128)S(1)}, f32[16,128,128]{2,1,0:T(8,128)S(1)}, f32[16,128,128]{2,1,0:T(8,128)S(1)}) custom-call(f32[128,2048]{1,0:T(8,128)} %bitcast.25, f32[3,8,16,2048]{3,2,1,0:T(8,128)} %bitcast.14, f32[16,8,16,128]{3,2,1,0:T(8,128)} %bitcast.19), custom_call_target="tpu_custom_call" | custom-call | flops 9437184 | bytes 9437184 | tf_op jit(solution)/shard_map/pallas_call | solution.py:18
  2.6 0.0 copy-start
  2.6 0.0 copy-start.1
  2.6 52.8 %all_to_all.10 = f32[128,3,16,128]{3,2,1,0:T(8,128)S(1)} all-to-all(f32[128,3,16,128]{3,2,1,0:T(8,128)S(1)} %bitcast.21), channel_id=1, replica_groups=mesh['py'=16,'pz'=8] {'py','pz'}, dimensions={0} | all-to-all | bytes 6291456 | tf_op jit(solution)/shard_map/all_to_all | solution.py:145
  55.4 0.0 copy-done
  55.4 0.0 copy-done.1
  55.4 1.5 %shard_map.51 = (f32[16,8,2,16,128]{4,3,2,1,0:T(8,128)S(1)}, f32[3,128,2048]{2,1,0:T(8,128)}, f32[2,128,2048]{2,1,0:T(8,128)S(1)}) custom-call(f32[16,8,3,16,128]{4,3,2,1,0:T(8,128)S(1)} %bitcast.16, f32[16,8,16,128]{3,2,1,0:T(8,128)S(1)} %bitcast.20, f32[16,128,128]{2,1,0:T(8,128)S(1)} %get-tuple-element.11.wz, f32[16,128,128]{2,1,0:T(8,128)S(1)} %get-tuple-element.12.wy, ...), custom_call_target="tpu_custom_call" | custom-call | flops 7340032 | bytes 7340032 | tf_op jit(solution)/shard_map/pallas_call | solution.py:18
  56.9 35.0 %all_to_all.11 = f32[128,2,16,128]{3,2,1,0:T(8,128)S(1)} all-to-all(f32[128,2,16,128]{3,2,1,0:T(8,128)S(1)} %bitcast.17), channel_id=1, replica_groups=mesh['py'=16,'pz'=8] {'py','pz'}, dimensions={0} | all-to-all | bytes 4194304 | tf_op jit(solution)/shard_map/all_to_all | solution.py:145
  91.9 1.7 %shard_map.52 = (f32[3,8,16,2048]{3,2,1,0:T(8,128)}, f32[16,8,16,128]{3,2,1,0:T(8,128)}) custom-call(f32[16,8,2,16,128]{4,3,2,1,0:T(8,128)S(1)} %bitcast.18, f32[16,8,2,16,128]{4,3,2,1,0:T(8,128)S(1)} %get-tuple-element.13.op, f32[2,8,16,2048]{3,2,1,0:T(8,128)S(1)} %bitcast.22, f32[3,8,16,2048]{3,2,1,0:T(8,128)} %bitcast.23), custom_call_target="tpu_custom_call", output_to_operand_aliasing={{0}: (3, {})} | custom-call | flops 3145728 | bytes 3145728 | tf_op jit(solution)/shard_map/pallas_call | solution.py:18
Async XLA Ops:
  2.6 52.8 %copy-start = (f32[3,1,128,2048]{3,2,1,0:T(8,128)S(1)}, f32[3,1,128,2048]{3,2,1,0:T(8,128)}, u32[]{:S(2)}) copy-start(f32[3,1,128,2048]{3,2,1,0:T(8,128)} %param.3) | copy-start | bytes 9437188
  2.6 52.8 %copy-start.1 = (f32[128,16,128]{2,1,0:T(8,128)S(1)}, f32[128,16,128]{2,1,0:T(8,128)}, u32[]{:S(2)}) copy-start(f32[128,16,128]{2,1,0:T(8,128)} %param.5) | copy-start | bytes 3145732
